TPU v7x, 32 devices: a whole 2x2x4 slice. The times are simulated.
32 devices in a mesh: batch: 16 (over z, y, core), gene: 2 (over x).
Axes of the slice: x: 2, y: 2, z: 4, core: 2. Of those that a mesh axis runs over, the one named last changes fastest.
Arguments:
- umi_counts: int32 [16384, 8192], P('batch', 'gene'), may hold values from 0 to 65535
- cell_donors: int32 [16384], P('batch'), may hold values from 0 to 127
- cell_types: int32 [16384], P('batch'), may hold values from 0 to 23
- live_cells: int32 [16], P('batch'), may hold values from 1 to 1024, 10240 in all
- dosages: int32 [128, 2048], P(None, 'batch'), may hold values from 0 to 2
Outputs:
- scores: bfloat16 [24, 8192, 2048], P(None, ('gene', 'batch'))
All inputs are finite; a program needn't handle non-finite values. No bound on the sum of `live_cells` on one device may be relied on, other than what follows from the above.
Results may differ from a plain program's by a relative error of at most 0.0069.
Values may be sent and summed in bfloat16 or wider, within the bound.
A program may use at most 128 MiB of HBM per device.

v0:
```python
import jax
import jax.numpy as jnp
from jax import lax
from jax.sharding import PartitionSpec as P

TYPES = 24
DONORS = 128


def one_hot_rows(group_ids, total_groups):
    columns = jnp.arange(total_groups, dtype=jnp.int32)
    return (group_ids[:, None] == columns[None, :]).astype(jnp.bfloat16)


def standardize_dosage(block_dosage):
    genotype = block_dosage.astype(jnp.float32)
    centred = genotype - jnp.mean(genotype, axis=0, keepdims=True)
    return (centred * lax.rsqrt(jnp.mean(centred * centred, axis=0, keepdims=True) + 1e-06)).astype(
        jnp.bfloat16
    )


def on_device(umi_counts, cell_donors, cell_types, live_cells, dosages):
    total_groups = TYPES * DONORS
    cell_slots = umi_counts.shape[0]
    genes_block = umi_counts.shape[1]
    batch_count = lax.axis_size("batch")
    genes_local = genes_block // batch_count
    slot_index = jnp.arange(cell_slots, dtype=jnp.int32)
    alive_mask = slot_index < live_cells[0]
    cell_group = jnp.where(alive_mask, cell_types * DONORS + cell_donors, -1)
    rounded = umi_counts.astype(jnp.bfloat16)
    exchanged = lax.all_to_all(rounded, "batch", split_axis=1, concat_axis=0, tiled=True)
    all_groups = lax.all_gather(cell_group, "batch", axis=0, tiled=True)
    block_rows = 4 * cell_slots
    block_turns = batch_count // 4

    def add_block(step_index, totals):
        block_counts = lax.dynamic_slice_in_dim(exchanged, step_index * block_rows, block_rows, 0)
        block_groups = lax.dynamic_slice_in_dim(all_groups, step_index * block_rows, block_rows, 0)
        table = one_hot_rows(block_groups, total_groups)
        return totals + lax.dot_general(
            block_counts, table, (((0,), (0,)), ((), ())), preferred_element_type=jnp.float32
        )

    pseudo = lax.fori_loop(
        0, block_turns, add_block, jnp.zeros((genes_local, total_groups), jnp.float32)
    )
    partial_library = jnp.sum(pseudo, axis=0)
    library = jnp.maximum(lax.psum(partial_library, ("batch", "gene")), 1.0)
    logged = jnp.log1p(10000.0 * pseudo / library[None, :]).reshape(genes_local, TYPES, DONORS)
    centred = logged - jnp.mean(logged, axis=2, keepdims=True)
    standard = (
        centred * lax.rsqrt(jnp.mean(centred * centred, axis=2, keepdims=True) + 1e-06)
    ).astype(jnp.bfloat16)
    standard_rows = jnp.transpose(standard, (1, 0, 2)).reshape(TYPES * genes_local, DONORS)
    factor = DONORS ** (-0.5)
    geno_local = standardize_dosage(dosages)
    geno_piece = lax.all_gather(geno_local, "batch", axis=1, tiled=True)
    product = jnp.dot(standard_rows, geno_piece, preferred_element_type=jnp.float32) * factor
    return product.reshape(TYPES, genes_local, geno_piece.shape[1]).astype(jnp.bfloat16)


def solution(mesh):
    placed = (P("batch", "gene"), P("batch"), P("batch"), P("batch"), P(None, "batch"))
    return jax.shard_map(
        on_device,
        mesh=mesh,
        in_specs=placed,
        out_specs=P(None, ("gene", "batch"), None),
        check_vma=False,
    )
```

profile of v0, /device:TPU:14, one launch (start us, length us, event | category | flops | bytes accessed | tf_op | source)
XLA Modules:
  0.0 357.4 jit_solution(3607183109049914522)
XLA Ops:
  0.0 9.0 %convert_element_type.21 = bf16[1024,4096]{1,0:T(8,128)(2,1)} convert(s32[1024,4096]{1,0:T(8,128)} %param.7) | non-fusion elementwise | flops 4194304 | bytes 25165824 | tf_op jit(solution)/shard_map/convert_element_type | solution.py:32
  9.0 7.4 %copy.16 = bf16[128,16,8,256]{3,2,0,1:T(8,128)(2,1)} copy(bf16[128,16,8,256]{3,2,1,0:T(8,128)(2,1)} %bitcast.19) | data formatting | bytes 16777216 | tf_op jit(solution)/shard_map/all_to_all | solution.py:33
  16.5 0.0 copy-start.2
  16.5 0.0 copy-start.3
  16.5 0.0 copy-start.1
  16.5 6.4 %all-to-all-start = ((bf16[1024,16,256]{2,0,1:T(8,128)(2,1)}), bf16[1024,16,256]{2,0,1:T(8,128)(2,1)}, u32[]{:S(2)}, u32[]{:S(2)}) async-start(bf16[1024,16,256]{2,0,1:T(8,128)(2,1)} %bitcast.20), calls=%async_computation | async-start | bytes 16777216 | tf_op jit(solution)/shard_map/all_to_all | solution.py:33
  23.5 0.0 copy-done.2
  23.5 0.0 copy-done.3
  23.5 191.0 %all_gather.6 = s32[16384]{0:T(1024)S(1)} all-gather(s32[1024]{0:T(1024)S(1)} %add_select_fusion), channel_id=1, replica_groups=mesh['batch'=16,'gene'=2] {'batch'}, dimensions={0}, use_global_device_ids=true | all-gather | bytes 69632 | tf_op jit(solution)/shard_map/all_gather | solution.py:34
  214.5 0.0 copy-done.1
  214.6 18.3 %all_gather.7 = bf16[128,2048]{1,0:T(8,128)(2,1)} all-gather(bf16[128,128]{1,0:T(8,128)(2,1)S(1)} %multiply_convert_fusion.2), channel_id=1, replica_groups=mesh['batch'=16,'gene'=2] {'batch'}, dimensions={1}, use_global_device_ids=true | all-gather | bytes 557056 | tf_op jit(solution)/shard_map/all_gather | solution.py:59
  232.9 0.0 all-to-all-done
  232.9 57.8 %while.14 = (s32[]{:T(128)}, f32[256,3072]{1,0:T(8,128)S(1)}, bf16[16384,256]{1,0:T(8,128)(2,1)}, s32[16384]{0:T(1024)S(1)}, s32[]{:T(128)}, /*index=5*/s32[]{:T(128)}, s32[]{:T(128)}, s32[]{:T(128)}) while((s32[]{:T(128)}, f32[256,3072]{1,0:T(8,128)S(1)}, bf16[16384,256]{1,0:T(8,128)(2,1)}, s32[16384]{0:T(1024)S(1)}, s32[]{:T(128)}, ...), condition=%wide.region_1.2_spmd.clone, body=%wide.region_0.1_spmd.clone.sunk | while | flops 6456606720 | bytes 8437917 | solution.py:46
  232.9 14.4 %fusion.11 = f32[256,3072]{1,0:T(8,128)S(1)} fusion(s32[4096]{0:T(1024)S(1)} %dynamic_slice.21, f32[256,3072]{1,0:T(8,128)S(1)} %get-tuple-element.142, bf16[16384,256]{1,0:T(8,128)(2,1)} %get-tuple-element.151, s32[]{:T(128)S(6)} %select_n.16, pred[]{:T(512)S(6)} %compare.3), kind=kOutput, calls=%fused_computation.3.clone.1 | convolution fusion | flops 6456606720 | bytes 8404997 | tf_op jit(solution)/shard_map/while/body/eval_jaxpr/dot_general | solution.py:42
  247.4 14.4 %fusion.11 = f32[256,3072]{1,0:T(8,128)S(1)} fusion(s32[4096]{0:T(1024)S(1)} %dynamic_slice.21, f32[256,3072]{1,0:T(8,128)S(1)} %get-tuple-element.142, bf16[16384,256]{1,0:T(8,128)(2,1)} %get-tuple-element.151, s32[]{:T(128)S(6)} %select_n.16, pred[]{:T(512)S(6)} %compare.3), kind=kOutput, calls=%fused_computation.3.clone.1 | convolution fusion | flops 6456606720 | bytes 8404997 | tf_op jit(solution)/shard_map/while/body/eval_jaxpr/dot_general | solution.py:42
  261.8 14.4 %fusion.11 = f32[256,3072]{1,0:T(8,128)S(1)} fusion(s32[4096]{0:T(1024)S(1)} %dynamic_slice.21, f32[256,3072]{1,0:T(8,128)S(1)} %get-tuple-element.142, bf16[16384,256]{1,0:T(8,128)(2,1)} %get-tuple-element.151, s32[]{:T(128)S(6)} %select_n.16, pred[]{:T(512)S(6)} %compare.3), kind=kOutput, calls=%fused_computation.3.clone.1 | convolution fusion | flops 6456606720 | bytes 8404997 | tf_op jit(solution)/shard_map/while/body/eval_jaxpr/dot_general | solution.py:42
  276.3 14.4 %fusion.11 = f32[256,3072]{1,0:T(8,128)S(1)} fusion(s32[4096]{0:T(1024)S(1)} %dynamic_slice.21, f32[256,3072]{1,0:T(8,128)S(1)} %get-tuple-element.142, bf16[16384,256]{1,0:T(8,128)(2,1)} %get-tuple-element.151, s32[]{:T(128)S(6)} %select_n.16, pred[]{:T(512)S(6)} %compare.3), kind=kOutput, calls=%fused_computation.3.clone.1 | convolution fusion | flops 6456606720 | bytes 8404997 | tf_op jit(solution)/shard_map/while/body/eval_jaxpr/dot_general | solution.py:42
  290.7 2.5 copy.12
  293.3 0.2 reduce_sum.45
  293.4 44.2 %psum.7 = f32[3072]{0:T(1024)S(1)} all-reduce(f32[3072]{0:T(1024)S(1)} %reduce_sum.45), channel_id=1, replica_groups=mesh['batch'=16,'gene'=2] {'batch','gene'}, use_global_device_ids=true, to_apply=%region_3.4 | all-reduce | flops 3072 | bytes 24576 | tf_op jit(solution)/shard_map/psum | solution.py:50
  337.7 3.1 divide_log-plus-one_fusion
  340.8 0.2 reduce_sum.46
  341.1 0.4 multiply_reduce_fusion
  341.5 1.6 fusion.5
  343.1 0.0 copy-start
  343.1 2.0 copy.13
  345.0 0.0 copy-done
  345.0 12.4 %multiply_convert_fusion = bf16[6144,2048]{1,0:T(8,128)(2,1)} fusion(bf16[6144,128]{1,0:T(8,128)(2,1)S(1)} %bitcast.21, bf16[128,2048]{1,0:T(8,128)(2,1)S(1)} %copy-done), kind=kOutput, calls=%fused_computation.6 | convolution fusion | flops 3246391296 | bytes 27262976 | tf_op jit(solution)/shard_map/dot_general | solution.py:60
  (14 shorter events, 0.2 us)
Async XLA Ops:
  16.5 7.0 %copy-start.2 = (s32[1024]{0:T(1024)S(1)}, s32[1024]{0:T(1024)}, u32[]{:S(2)}) copy-start(s32[1024]{0:T(1024)} %param.8) | copy-start | bytes 12292
  16.5 7.0 %copy-start.3 = (s32[1024]{0:T(1024)S(1)}, s32[1024]{0:T(1024)}, u32[]{:S(2)}) copy-start(s32[1024]{0:T(1024)} %param.9) | copy-start | bytes 12292
  16.5 198.0 %copy-start.1 = (s32[128,128]{1,0:T(8,128)S(1)}, s32[128,128]{1,0:T(8,128)}, u32[]{:S(2)}) copy-start(s32[128,128]{1,0:T(8,128)} %param.11) | copy-start | bytes 196612
  16.5 216.4 %all-to-all-start = ((bf16[1024,16,256]{2,0,1:T(8,128)(2,1)}), bf16[1024,16,256]{2,0,1:T(8,128)(2,1)}, u32[]{:S(2)}, u32[]{:S(2)}) async-start(bf16[1024,16,256]{2,0,1:T(8,128)(2,1)} %bitcast.20), calls=%async_computation | async-start | bytes 16777216 | tf_op jit(solution)/shard_map/all_to_all | solution.py:33
  343.1 2.0 copy-start
where the time goes:
time: 358 us; the launch traced here: 357 us
  blocking collectives  253 us (71%)
  matrix products  70 us (20%)
  other arithmetic  14.7 us (4%)
  local copies, waits for them, and re-layouts  12 us (3%)
  starting transfers between devices  6.37 us (2%)
    all_gather x1, blocking collectives, on_device(): all_groups = lax.all_gather(cell_group, 'batch', axis=0, tiled=True)  191 us
    dot_general x4, matrix products, add_block(): lax.dot_general(block_counts, table, (((0,), (0,)), ((), ())), preferred_...  57.6 us
    psum x1, blocking collectives, on_device(): library = jnp.maximum(lax.psum(partial_library, ('batch', 'gene')), 1.0)  44.2 us
    all_gather x1, blocking collectives, on_device(): geno_piece = lax.all_gather(geno_local, 'batch', axis=1, tiled=True)  18.3 us
    dot_general x1, matrix products, on_device(): jnp.dot(standard_rows, geno_piece, preferred_element_type=jnp.float32)  12.4 us
    convert_element_type x1, other arithmetic, on_device(): rounded = umi_counts.astype(jnp.bfloat16)  9.05 us
    all_to_all x1, local copies, waits for them, and re-layouts, on_device(): lax.all_to_all(rounded, 'batch', split_axis=1, concat_axis=0, tiled=True)  7.43 us
  transfers between devices with their start and end apart: 1, of which 0 were waited for; matrix products, arithmetic and copies ran while one was open for 0% of the time, Pallas kernels for 0%

commit v1 on v0

--- a/solution.py
+++ b/solution.py
@@ -5,6 +5,12 @@
 
 TYPES = 24
 DONORS = 128
+
+
+def summed_here(array, mesh_axis):
+    shards = lax.all_gather(array, mesh_axis, axis=0, tiled=False)
+    acc = shards.sum(axis=0)
+    return acc
 
 
 def one_hot_rows(group_ids, total_groups):
@@ -47,7 +53,7 @@
         0, block_turns, add_block, jnp.zeros((genes_local, total_groups), jnp.float32)
     )
     partial_library = jnp.sum(pseudo, axis=0)
-    library = jnp.maximum(lax.psum(partial_library, ("batch", "gene")), 1.0)
+    library = jnp.maximum(summed_here(partial_library, ("batch", "gene")), 1.0)
     logged = jnp.log1p(10000.0 * pseudo / library[None, :]).reshape(genes_local, TYPES, DONORS)
     centred = logged - jnp.mean(logged, axis=2, keepdims=True)
     standard = (

time: 358 us -> 387 us (1.081)
  the two profiles are of different devices: /device:TPU:14 before, /device:TPU:0 now
where the time goes in v1:
time: 387 us
  blocking collectives  282 us (73%)
  matrix products  70 us (18%)
  other arithmetic  14.7 us (4%)
  local copies, waits for them, and re-layouts  12.1 us (3%)
  starting transfers between devices  7.6 us (2%)
    all_gather x1, blocking collectives, on_device(): all_groups = lax.all_gather(cell_group, 'batch', axis=0, tiled=True)  151 us
    all_gather x1, blocking collectives, summed_here(): shards = lax.all_gather(array, mesh_axis, axis=0, tiled=False)  67 us
    all_gather x1, blocking collectives, on_device(): geno_piece = lax.all_gather(geno_local, 'batch', axis=1, tiled=True)  63.4 us
    dot_general x4, matrix products, add_block(): lax.dot_general(block_counts, table, (((0,), (0,)), ((), ())), preferred_...  57.6 us
    dot_general x1, matrix products, on_device(): jnp.dot(standard_rows, geno_piece, preferred_element_type=jnp.float32)  12.4 us
    convert_element_type x1, other arithmetic, on_device(): rounded = umi_counts.astype(jnp.bfloat16)  9.05 us
  transfers between devices with their start and end apart: 1, of which 0 were waited for; matrix products, arithmetic and copies ran while one was open for 0% of the time, Pallas kernels for 0%

profile of v1, /device:TPU:0, one launch (start us, length us, event | category | flops | bytes accessed | tf_op | source)
XLA Modules:
  0.0 386.9 jit_solution(691277206863017395)
XLA Ops:
  0.0 9.0 %convert_element_type.21 = bf16[1024,4096]{1,0:T(8,128)(2,1)} convert(s32[1024,4096]{1,0:T(8,128)} %param.7) | non-fusion elementwise | flops 4194304 | bytes 25165824 | tf_op jit(solution)/shard_map/convert_element_type | solution.py:38
  9.0 7.4 %copy.19 = bf16[128,16,8,256]{3,2,0,1:T(8,128)(2,1)} copy(bf16[128,16,8,256]{3,2,1,0:T(8,128)(2,1)} %bitcast.19) | data formatting | bytes 16777216 | tf_op jit(solution)/shard_map/all_to_all | solution.py:39
  16.5 0.0 copy-start.2
  16.5 0.0 copy-start.3
  16.5 0.0 copy-start.1
  16.5 7.6 %all-to-all-start = ((bf16[1024,16,256]{2,0,1:T(8,128)(2,1)}), bf16[1024,16,256]{2,0,1:T(8,128)(2,1)}, u32[]{:S(2)}, u32[]{:S(2)}) async-start(bf16[1024,16,256]{2,0,1:T(8,128)(2,1)} %bitcast.20), calls=%async_computation | async-start | bytes 16777216 | tf_op jit(solution)/shard_map/all_to_all | solution.py:39
  24.7 0.0 copy-done.2
  24.8 0.0 copy-done.3
  24.8 151.2 %all_gather.12 = s32[16384]{0:T(1024)S(1)} all-gather(s32[1024]{0:T(1024)S(1)} %add_select_fusion), channel_id=1, replica_groups=mesh['batch'=16,'gene'=2] {'batch'}, dimensions={0}, use_global_device_ids=true | all-gather | bytes 69632 | tf_op jit(solution)/shard_map/all_gather | solution.py:40
  176.0 0.0 copy-done.1
  176.1 63.4 %all_gather.15 = bf16[128,2048]{1,0:T(8,128)(2,1)} all-gather(bf16[128,128]{1,0:T(8,128)(2,1)S(1)} %multiply_convert_fusion.2), channel_id=1, replica_groups=mesh['batch'=16,'gene'=2] {'batch'}, dimensions={1}, use_global_device_ids=true | all-gather | bytes 557056 | tf_op jit(solution)/shard_map/all_gather | solution.py:65
  239.6 0.0 all-to-all-done
  239.6 57.8 %while.14 = (s32[]{:T(128)}, f32[256,3072]{1,0:T(8,128)S(1)}, bf16[16384,256]{1,0:T(8,128)(2,1)}, s32[16384]{0:T(1024)S(1)}, s32[]{:T(128)}, /*index=5*/s32[]{:T(128)}, s32[]{:T(128)}, s32[]{:T(128)}) while((s32[]{:T(128)}, f32[256,3072]{1,0:T(8,128)S(1)}, bf16[16384,256]{1,0:T(8,128)(2,1)}, s32[16384]{0:T(1024)S(1)}, s32[]{:T(128)}, ...), condition=%wide.region_1.2_spmd.clone, body=%wide.region_0.1_spmd.clone.sunk | while | flops 6456606720 | bytes 8437917 | solution.py:52
  239.6 14.4 %fusion.11 = f32[256,3072]{1,0:T(8,128)S(1)} fusion(s32[4096]{0:T(1024)S(1)} %dynamic_slice.21, f32[256,3072]{1,0:T(8,128)S(1)} %get-tuple-element.142, bf16[16384,256]{1,0:T(8,128)(2,1)} %get-tuple-element.151, s32[]{:T(128)S(6)} %select_n.16, pred[]{:T(512)S(6)} %compare.3), kind=kOutput, calls=%fused_computation.3.clone.1 | convolution fusion | flops 6456606720 | bytes 8404997 | tf_op jit(solution)/shard_map/while/body/eval_jaxpr/dot_general | solution.py:48
  254.0 14.4 %fusion.11 = f32[256,3072]{1,0:T(8,128)S(1)} fusion(s32[4096]{0:T(1024)S(1)} %dynamic_slice.21, f32[256,3072]{1,0:T(8,128)S(1)} %get-tuple-element.142, bf16[16384,256]{1,0:T(8,128)(2,1)} %get-tuple-element.151, s32[]{:T(128)S(6)} %select_n.16, pred[]{:T(512)S(6)} %compare.3), kind=kOutput, calls=%fused_computation.3.clone.1 | convolution fusion | flops 6456606720 | bytes 8404997 | tf_op jit(solution)/shard_map/while/body/eval_jaxpr/dot_general | solution.py:48
  268.5 14.4 %fusion.11 = f32[256,3072]{1,0:T(8,128)S(1)} fusion(s32[4096]{0:T(1024)S(1)} %dynamic_slice.21, f32[256,3072]{1,0:T(8,128)S(1)} %get-tuple-element.142, bf16[16384,256]{1,0:T(8,128)(2,1)} %get-tuple-element.151, s32[]{:T(128)S(6)} %select_n.16, pred[]{:T(512)S(6)} %compare.3), kind=kOutput, calls=%fused_computation.3.clone.1 | convolution fusion | flops 6456606720 | bytes 8404997 | tf_op jit(solution)/shard_map/while/body/eval_jaxpr/dot_general | solution.py:48
  282.9 14.4 %fusion.11 = f32[256,3072]{1,0:T(8,128)S(1)} fusion(s32[4096]{0:T(1024)S(1)} %dynamic_slice.21, f32[256,3072]{1,0:T(8,128)S(1)} %get-tuple-element.142, bf16[16384,256]{1,0:T(8,128)(2,1)} %get-tuple-element.151, s32[]{:T(128)S(6)} %select_n.16, pred[]{:T(512)S(6)} %compare.3), kind=kOutput, calls=%fused_computation.3.clone.1 | convolution fusion | flops 6456606720 | bytes 8404997 | tf_op jit(solution)/shard_map/while/body/eval_jaxpr/dot_general | solution.py:48
  297.4 2.5 copy.15
  299.9 0.2 reduce_sum.54
  300.1 67.0 %all-gather = f32[98304]{0:T(1024)S(1)} all-gather(f32[3072]{0:T(1024)S(1)} %reduce_sum.54), channel_id=2, replica_groups=mesh['batch'=16,'gene'=2] {'batch','gene'}, dimensions={0}, use_global_device_ids=true | all-gather | bytes 405504 | tf_op jit(solution)/shard_map/all_gather | solution.py:11
  367.1 0.1 reshape.41
  367.2 3.1 divide_log-plus-one_fusion
  370.3 0.2 reduce_sum.56
  370.6 0.4 multiply_reduce_fusion
  371.0 1.6 fusion.5
  372.6 0.0 copy-start
  372.6 2.0 copy.16
  374.6 0.0 copy-done
  374.6 12.4 %multiply_convert_fusion = bf16[6144,2048]{1,0:T(8,128)(2,1)} fusion(bf16[6144,128]{1,0:T(8,128)(2,1)S(1)} %bitcast.21, bf16[128,2048]{1,0:T(8,128)(2,1)S(1)} %copy-done), kind=kOutput, calls=%fused_computation.6 | convolution fusion | flops 3246391296 | bytes 27262976 | tf_op jit(solution)/shard_map/dot_general | solution.py:66
  (15 shorter events, 0.2 us)
Async XLA Ops:
  16.5 8.3 %copy-start.2 = (s32[1024]{0:T(1024)S(1)}, s32[1024]{0:T(1024)}, u32[]{:S(2)}) copy-start(s32[1024]{0:T(1024)} %param.8) | copy-start | bytes 12292
  16.5 8.3 %copy-start.3 = (s32[1024]{0:T(1024)S(1)}, s32[1024]{0:T(1024)}, u32[]{:S(2)}) copy-start(s32[1024]{0:T(1024)} %param.9) | copy-start | bytes 12292
  16.5 159.5 %copy-start.1 = (s32[128,128]{1,0:T(8,128)S(1)}, s32[128,128]{1,0:T(8,128)}, u32[]{:S(2)}) copy-start(s32[128,128]{1,0:T(8,128)} %param.11) | copy-start | bytes 196612
  16.5 223.1 %all-to-all-start = ((bf16[1024,16,256]{2,0,1:T(8,128)(2,1)}), bf16[1024,16,256]{2,0,1:T(8,128)(2,1)}, u32[]{:S(2)}, u32[]{:S(2)}) async-start(bf16[1024,16,256]{2,0,1:T(8,128)(2,1)} %bitcast.20), calls=%async_computation | async-start | bytes 16777216 | tf_op jit(solution)/shard_map/all_to_all | solution.py:39
  372.6 2.0 copy-start
